TPU v7x, 32 devices: a whole 2x2x4 slice. The times are simulated.
32 devices in a mesh: rows: 16 (over z, x, core), cols: 2 (over y).
Axes of the slice: x: 2, y: 2, z: 4, core: 2. Of those that a mesh axis runs over, the one named last changes fastest.
Arguments:
- columns: float32 [512, 16384], P('cols', 'rows'), may hold values from -200 to 200
Outputs:
- orthonormal: float32 [256, 16384], P('cols', 'rows')
- triangle: float32 [256, 512], P('cols')
- trailing: float32 [256, 16384], P('cols', 'rows')
All inputs are finite; a program needn't handle non-finite values.
Results may differ from a plain program's by a relative error of at most 0.00008.
Values sent between devices are 32-bit elements; how exact they have to be, the bound alone decides.
A program may use at most 64 MiB of HBM per device.

v0:
```python
import math

import jax
import jax.numpy as jnp
from jax import lax
from jax.sharding import PartitionSpec as P

PANEL = 128


precise = lax.Precision.HIGHEST


def product(left, right):
    return jnp.dot(left, right, precision=precise, preferred_element_type=jnp.float32)


def inverse_lower(lower):
    identity = jnp.eye(lower.shape[0], dtype=lower.dtype)
    return lax.linalg.triangular_solve(lower, identity, left_side=True, lower=True)


def summed(partial_term):
    return lax.psum(partial_term, "rows")


def shards(columns):
    col_count = lax.axis_size("cols")
    col_index = lax.axis_index("cols")
    scaling = math.sqrt(columns.shape[1] * lax.axis_size("rows"))
    local_rows = lax.all_gather(columns, "cols", axis=0, tiled=True)
    panel_count = 2 * PANEL
    leading = local_rows[:panel_count]
    gram_strip = summed(product(leading, local_rows.T))
    lower_both = jnp.linalg.cholesky(gram_strip[:, :panel_count])
    inverse_both = inverse_lower(lower_both)
    orthonormal = product(inverse_both, leading)
    coupling = product(inverse_both, gram_strip[:, panel_count:])
    trailing = local_rows[panel_count:] - product(coupling.T, orthonormal)
    triangle = jnp.concatenate([lower_both.T, coupling], axis=1)
    orthonormal = orthonormal * scaling
    triangle = triangle / scaling
    tri_rows = triangle.shape[0] // col_count
    triangle_own = lax.dynamic_slice_in_dim(triangle, col_index * tri_rows, tri_rows, 0)
    ortho_rows = orthonormal.shape[0] // col_count
    trail_rows = trailing.shape[0] // col_count
    ortho_own = lax.dynamic_slice_in_dim(orthonormal, col_index * ortho_rows, ortho_rows, 0)
    trailing_own = lax.dynamic_slice_in_dim(trailing, col_index * trail_rows, trail_rows, 0)
    return (ortho_own, triangle_own, trailing_own)


def solution(mesh):
    placed = (P("cols", "rows"),)
    return jax.shard_map(
        shards,
        mesh=mesh,
        in_specs=placed,
        out_specs=(P("cols", "rows"), P("cols", None), P("cols", "rows")),
        check_vma=False,
    )
```

profile of v0, /device:TPU:0, one launch (start us, length us, event | category | flops | bytes accessed | tf_op | source)
XLA Modules:
  0.0 215.3 jit_solution(8405446448835220945)
XLA Ops:
  7.2 0.0 all-gather.2.cloned.1.call-start
  7.2 0.7 all-gather.2.cloned.1.call-update
  7.9 0.0 all-reduce.3.cloned.1.call-start
  7.9 37.4 %all-gather.2.cloned.1.call-done = f32[512,1024]{1,0:T(8,128)} async-done(((f32[256,1024]{1,0:T(8,128)}), f32[512,1024]{1,0:T(8,128)}) %all-gather.2.cloned.1.call-update) | async-done | bytes 2097168 | tf_op jit(solution)/shard_map/all_gather | solution.py:31
  45.4 4.5 %fusion.2 = f32[256,512]{0,1:T(8,128)} fusion(f32[512,1024]{1,0:T(8,128)} %all-gather.2.cloned.1.call-done), kind=kOutput, calls=%fused_computation.6 | convolution fusion | flops 1610612736 | bytes 3670016 | tf_op jit(solution)/shard_map/dot_general | solution.py:15
  49.9 0.0 all-reduce.3.cloned.1.call-update
  50.0 90.8 %all-reduce.3.cloned.1.call-done = f32[256,512]{0,1:T(8,128)} async-done(((f32[256,512]{0,1:T(8,128)}), f32[256,512]{0,1:T(8,128)}) %all-reduce.3.cloned.1.call-update) | async-done | bytes 524304 | tf_op jit(solution)/shard_map/psum | solution.py:24
  140.8 1.0 slice.71
  141.7 0.1 copy.5
  141.9 1.0 fusion.8
  142.9 11.7 %cholesky.50 = f32[128,128]{1,0:T(8,128)S(1)} custom-call(f32[128,128]{1,0:T(8,128)S(1)} %cholesky.118), custom_call_target="Cholesky" | custom-call | tf_op jit(solution)/shard_map/jit(cholesky)/cholesky | solution.py:35
  154.6 9.8 %custom-call.14 = f32[1,128,128]{1,2,0:T(8,128)S(1)} custom-call(f32[1,128,128]{2,1,0:T(8,128)S(1)} %get-tuple-element.29), custom_call_target="InvertDiagBlocksLowerTriangular" | custom-call | tf_op jit(solution)/shard_map/jit(cholesky)/cholesky | solution.py:35
  164.5 0.2 constant_dynamic-update-slice_fusion
  164.7 0.3 convolution_subtract_fusion.1
  165.0 11.8 %cholesky.105 = f32[128,128]{1,0:T(8,128)S(1)} custom-call(f32[128,128]{1,0:T(8,128)S(1)} %convolution_subtract_fusion.1), custom_call_target="Cholesky" | custom-call | tf_op jit(solution)/shard_map/jit(cholesky)/cholesky | solution.py:35
  176.8 0.6 compare_reduce_fusion
  178.8 0.1 triangular_solve.63
  178.9 4.0 %while.1 = (s32[]{:T(128)}, f32[256,256]{1,0:T(8,128)S(1)}, s32[2,2]{1,0:T(2,128)S(1)}, f32[2,128,128]{2,1,0:T(8,128)S(1)}, s32[]{:T(128)}) while((s32[]{:T(128)}, f32[256,256]{1,0:T(8,128)S(1)}, s32[2,2]{1,0:T(2,128)S(1)}, f32[2,128,128]{2,1,0:T(8,128)S(1)}, s32[]{:T(128)}) %tuple.29), condition=%wide.while_cond, body=%wide.while_body.sunk | while | flops 2 | bytes 131189 | solution.py:20
  178.9 0.6 fusion.30
  179.5 1.4 bitcast_dynamic-update-slice_fusion.2
  180.9 0.6 fusion.30
  181.5 1.4 bitcast_dynamic-update-slice_fusion.2
  182.9 19.7 %custom-call.15 = f32[2,128,128]{1,2,0:T(8,128)S(1)} custom-call(f32[2,128,128]{2,1,0:T(8,128)S(1)} %get-tuple-element.10), custom_call_target="InvertDiagBlocksLowerTriangular" | custom-call | tf_op jit(solution)/shard_map/triangular_solve | solution.py:20
  202.6 0.3 fusion.11
  202.8 0.3 convolution_subtract_fusion
  203.1 0.3 fusion.14
  203.4 1.0 fusion
  204.5 0.8 dynamic-slice_multiply_fusion
  205.3 0.4 fusion.6
  205.7 1.0 fusion.21
  206.8 0.8 copy.6
  207.7 0.9 dynamic-slice_subtract_fusion
  (17 shorter events, 0.2 us)
Async XLA Ops:
  7.2 38.2 %all-gather.2.cloned.1.call-start = ((), (), s32[]{:S(2)}) async-start(), calls=%async_computation | async-start | bytes 3145728 | tf_op jit(solution)/shard_map/all_gather | solution.py:31
  7.9 132.9 %all-reduce.3.cloned.1.call-start = ((), (), s32[]{:S(2)}) async-start(), calls=%async_computation.1 | async-start | bytes 1048576 | tf_op jit(solution)/shard_map/psum | solution.py:24
  142.9 60.5 %copy-start = (f32[512,1024]{1,0:T(8,128)S(1)}, f32[512,1024]{1,0:T(8,128)}, u32[]{:S(2)}) copy-start(f32[512,1024]{1,0:T(8,128)} %all-gather.2.cloned.1.call-done) | copy-start | bytes 6291460
  202.8 2.5 %copy-start.1 = (f32[256,512]{0,1:T(8,128)S(1)}, f32[256,512]{0,1:T(8,128)}, u32[]{:S(2)}) copy-start(f32[256,512]{0,1:T(8,128)} %all-reduce.3.cloned.1.call-done) | copy-start | bytes 1572868
  205.3 2.3 %slice-start = ((f32[512,1024]{1,0:T(8,128)}), f32[256,1024]{1,0:T(8,128)S(1)}, s32[]{:S(2)}) async-start(f32[512,1024]{1,0:T(8,128)} %all-gather.2.cloned.1.call-done), calls=%async_computation.2 | async-start | bytes 2097152 | tf_op jit(solution)/shard_map/slice | solution.py:39
Sparse Core Ops, SparseCore 0:
  9.5 35.8 all-gather.1
  50.1 90.6 all-reduce.2
where the time goes:
time: 216 us; the launch traced here: 215 us
  waiting for transfers between devices  129 us (60%)
  other arithmetic  56.5 us (26%)
  between operations  15.5 us (7%)
  matrix products  8.32 us (4%)
  local copies, waits for them, and re-layouts  5.99 us (3%)
    psum x1, waiting for transfers between devices, summed(): return lax.psum(partial_term, 'rows')  90.8 us
    all_gather x1, waiting for transfers between devices, shards(): local_rows = lax.all_gather(columns, 'cols', axis=0, tiled=True)  37.4 us
    another operation x6, other arithmetic, shards(): lower_both = jnp.linalg.cholesky(gram_strip[:, :panel_count])  34 us
    another operation x2, other arithmetic, inverse_lower(): lax.linalg.triangular_solve(lower, identity, left_side=True, lower=True)  19.7 us
    dot_general x4, matrix products, product(): jnp.dot(left, right, precision=precise, preferred_element_type=jnp.float32)  7.01 us
  transfers between devices with their start and end apart: 2, of which 2 were waited for; matrix products, arithmetic and copies ran while one was open for 0% of the time, Pallas kernels for 0%

commit v1 on v0

v1 whole, which is shorter than its diff:
```python
import functools
import math

import jax
import jax.numpy as jnp
from jax import lax
from jax.experimental import pallas as pl
from jax.experimental.pallas import tpu as pltpu
from jax.sharding import PartitionSpec as P

PANEL = 128
STRIP = 16
MESH = pl.DeviceIdType.MESH

precise = lax.Precision.HIGHEST


def product(left, right):
    return jnp.dot(left, right, precision=precise, preferred_element_type=jnp.float32)


def contract(left, right, dims):
    return lax.dot_general(
        left, right, (dims, ((), ())), precision=precise, preferred_element_type=jnp.float32
    )


def across_rows(left, right):
    return contract(left, right, ((1,), (1,)))


def pieces(value):
    first = value.astype(jnp.bfloat16)
    rest = value - first.astype(jnp.float32)
    second = rest.astype(jnp.bfloat16)
    third = (rest - second.astype(jnp.float32)).astype(jnp.bfloat16)
    return first, second, third


def strip_update(left, right):
    a, b, c = pieces(left)
    d, e, f = pieces(right)
    lhs = jnp.concatenate([a, a, b, a, c, b], axis=0)
    rhs = jnp.concatenate([d, e, d, f, d, e], axis=0)
    return lax.dot_general(
        lhs, rhs, (((0,), (0,)), ((), ())), preferred_element_type=jnp.float32
    )


def eliminate(ref, hooks):
    size = ref.shape[0]
    lanes = size
    parts = ref.shape[1] // lanes
    below = lax.broadcasted_iota(jnp.int32, (STRIP, lanes), 0)
    for s in range(size // STRIP):
        at = s * STRIP
        rows = [ref[at:at + STRIP, q * lanes:(q + 1) * lanes] for q in range(parts)]
        cols = [
            jnp.broadcast_to(rows[0][:, at + j:at + j + 1], (STRIP, lanes))
            for j in range(STRIP)
        ]
        for i in range(STRIP):
            pivot = cols[i][i:i + 1]
            inv = lax.rsqrt(pivot)
            inv = inv * (1.5 - 0.5 * pivot * inv * inv)
            col = cols[i] * inv
            coef = jnp.where(below > i, col, 0.0)
            for j in range(i + 1, STRIP):
                cols[j] = cols[j] - coef * col[j:j + 1]
            for q in range(parts):
                row = rows[q][i:i + 1] * inv
                rows[q] = jnp.where(below == i, row, rows[q] - coef * row)
        for q in range(parts):
            ref[at:at + STRIP, q * lanes:(q + 1) * lanes] = rows[q]
        after = at + STRIP
        if after < size:
            update = strip_update(rows[0], jnp.concatenate(rows, axis=1))
            ref[after:, :] = ref[after:, :] - update[after:, :]
        if s in hooks:
            hooks[s]()


def kernel(row_count, scaling, x_ref, ortho_ref, tri_ref, trail_ref,
           xs, a2, part, gram, pair_in, ring_in, both, first, second,
           xy, xy_pair, xy_ring, send, recv_x, recv_pair, recv_ring, recv_all,
           recv_half, recv_y):
    r = lax.axis_index("rows")
    c = lax.axis_index("cols")
    other = 1 - c
    parity = lax.rem(r, 2)
    h = r // 2
    mates = row_count // 2
    partner = (r + 1 - 2 * parity, c)
    across = (r, other)
    size = PANEL

    def mate(k):
        idx = lax.rem(h + k, mates)
        return idx, (idx * 2 + parity, c)

    barrier = pltpu.get_barrier_semaphore()
    for target in [partner, across] + [mate(k)[1] for k in range(1, mates)]:
        pl.semaphore_signal(barrier, inc=1, device_id=target, device_id_type=MESH)
    pl.semaphore_wait(barrier, mates + 1)

    def push(src, dst, send_sem, recv_sem, target):
        return pltpu.make_async_remote_copy(
            src_ref=src, dst_ref=dst, send_sem=send_sem, recv_sem=recv_sem,
            device_id=target, device_id_type=MESH)

    quarter = size // 2

    def x_copy(q):
        return push(x_ref.at[pl.ds(q * quarter, quarter)],
                    xs.at[pl.ds(q * quarter, quarter)],
                    send.at[q], recv_x.at[q], across)

    def a2_copy(q):
        return push(x_ref.at[pl.ds(q * quarter, quarter)],
                    a2.at[pl.ds(q * quarter, quarter)],
                    send.at[q], recv_x.at[q], across)

    @pl.when(c == 0)
    def _():
        x_copy(0).start()
        x_copy(1).start()

    @pl.when(c == 1)
    def _():
        a2_copy(0).start()
        a2_copy(1).start()
        a2[...] = x_ref[size:, :]

    def spread(base, full, pair_buf, ring_buf, tag):
        half = full.shape[0] // 2
        chunk = half // mates
        mine = pl.ds(parity * half, half)
        his = pl.ds((1 - parity) * half, half)
        own = pl.ds(pl.multiple_of(parity * half + h * chunk, 8), chunk)

        def pair_copy():
            return push(full.at[his], pair_buf, send.at[base],
                        recv_pair.at[tag], partner)

        def ring_copy(k):
            idx, target = mate(k)
            return push(
                full.at[pl.ds(pl.multiple_of(parity * half + idx * chunk, 8), chunk)],
                ring_buf.at[k], send.at[base + k], recv_ring.at[tag * mates + k], target)

        def gather_copy(dst, k):
            return push(dst.at[own], dst.at[own], send.at[base + mates + k],
                        recv_all.at[tag * mates + k], mate(k)[1])

        def gather_wait(dst, k):
            idx = lax.rem(h + mates - k, mates)
            there = pl.ds(pl.multiple_of(parity * half + idx * chunk, 8), chunk)
            push(dst.at[there], dst.at[there], send.at[base + mates + k],
                 recv_all.at[tag * mates + k], mate(k)[1]).wait_recv()

        def half_copy(dst):
            return push(dst.at[mine], dst.at[mine], send.at[base + 2 * mates],
                        recv_half.at[tag], partner)

        def half_wait(dst):
            push(dst.at[his], dst.at[his], send.at[base + 2 * mates],
                 recv_half.at[tag], partner).wait_recv()

        def start_pair():
            pair_copy().start()

        def start_ring():
            pair_copy().wait_recv()
            full[mine] = full[mine] + pair_buf[...]
            for k in range(1, mates):
                ring_copy(k).start()

        def finish_ring(dst):
            for k in range(1, mates):
                ring_copy(k).wait_recv()
            total = full[own]
            for k in range(1, mates):
                total = total + ring_buf[k]
            dst[own] = total

        def drain_scatter():
            pair_copy().wait_send()
            for k in range(1, mates):
                ring_copy(k).wait_send()

        def start_gather(dst):
            for k in range(1, mates):
                gather_copy(dst, k).start()

        def start_half(dst):
            for k in range(1, mates):
                gather_wait(dst, k)
            half_copy(dst).start()

        def finish(dst):
            half_wait(dst)

        def drain_gather(dst):
            for k in range(1, mates):
                gather_copy(dst, k).wait_send()
            half_copy(dst).wait_send()

        return (start_pair, start_ring, finish_ring, drain_scatter, start_gather,
                start_half, finish, drain_gather, own)

    base_g = 4
    (g_pair, g_ring, g_sum, g_drain, g_gather, g_half, g_finish, g_drain_all,
     g_own) = spread(base_g, part, pair_in, ring_in, 0)
    base_y = base_g + 2 * mates + 2
    y_send = send.at[base_g + 2 * mates + 1]

    def chunk_copy():
        return push(gram.at[g_own], gram.at[g_own], y_send, recv_y.at[0], across)

    @pl.when(c == 0)
    def _():
        part[:2 * size] = across_rows(x_ref[...], x_ref[:size])
        part[2 * size:] = across_rows(x_ref[size:, :], x_ref[size:, :])
        low = part[size:2 * size]
        part[size:2 * size] = low.T
        g_pair()
        xs[...] = x_ref[...]
        g_ring()
        g_sum(gram)
        chunk_copy().start()
        x_copy(2).start()
        x_copy(3).start()

    @pl.when(c == 1)
    def _():
        chunk_copy().wait_recv()

    g_gather(gram)
    g_half(gram)
    g_finish(gram)

    eye = (lax.broadcasted_iota(jnp.int32, (size, size), 0)
           == lax.broadcasted_iota(jnp.int32, (size, size), 1)).astype(jnp.float32)
    first[:, :size] = gram[:size]
    first[:, size:2 * size] = gram[size:2 * size]
    first[:, 2 * size:] = eye
    eliminate(first, {})

    @pl.when(c == 0)
    def _():
        a2_copy(0).wait_recv()
        a2_copy(1).wait_recv()

    @pl.when(c == 1)
    def _():
        for q in range(4):
            x_copy(q).wait_recv()

    (y_pair, y_ring, y_sum, y_drain, y_gather, y_half, y_finish, y_drain_all,
     _own) = spread(base_y, xy, xy_pair, xy_ring, 1)
    xy[...] = across_rows(xs[...], a2[...])
    y_pair()

    upper = first[:, size:2 * size]
    cross = contract(upper, first[:, size:], ((0,), (0,)))
    second[:, :size] = gram[2 * size:] - cross[:, :size]
    second[:, size:2 * size] = -cross[:, size:]
    second[:, 2 * size:] = eye

    mine_xy = both.at[c]

    def swap_copy():
        return push(both.at[c], both.at[c], send.at[base_y + 2 * mates + 1],
                    recv_y.at[1], across)

    def swap_wait():
        push(both.at[other], both.at[other], send.at[base_y + 2 * mates + 1],
             recv_y.at[1], across).wait_recv()

    def hook_sum():
        y_sum(mine_xy)
        y_gather(mine_xy)

    def hook_swap():
        y_finish(mine_xy)
        swap_copy().start()

    eliminate(second, {0: y_ring, 3: hook_sum, 6: lambda: y_half(mine_xy), 7: hook_swap})

    inv00 = first[:, 2 * size:]
    inv1 = second[:, size:]
    mine = both[c]
    coup0 = product(inv00, mine[:size])
    coup1 = product(inv1, mine)
    weights = contract(coup1, inv1, ((0,), (0,)))
    weights0 = weights[:, :size] + contract(coup0, inv00, ((0,), (0,)))
    trail_ref[...] = a2[...] - (product(weights0, xs[:size]) + product(weights[:, size:], xs[size:]))

    @pl.when(c == 0)
    def _():
        ortho_ref[...] = product(inv00, xs[:size]) * scaling

    @pl.when(c == 1)
    def _():
        ortho_ref[...] = product(inv1, xs[...]) * scaling

    swap_wait()
    keep = (lax.broadcasted_iota(jnp.int32, (size, size), 0)
            <= lax.broadcasted_iota(jnp.int32, (size, size), 1))

    @pl.when(c == 0)
    def _():
        tri_ref[:, :size] = jnp.where(keep, first[:, :size], 0.0) / scaling
        tri_ref[:, size:2 * size] = first[:, size:2 * size] / scaling
        for k in range(2):
            tri_ref[:, (2 + k) * size:(3 + k) * size] = (
                product(inv00, both[k][:size]) / scaling)
        for q in range(4):
            x_copy(q).wait_send()
        g_drain()
        chunk_copy().wait_send()

    @pl.when(c == 1)
    def _():
        tri_ref[:, :size] = jnp.zeros((size, size), jnp.float32)
        tri_ref[:, size:2 * size] = jnp.where(keep, second[:, :size], 0.0) / scaling
        for k in range(2):
            tri_ref[:, (2 + k) * size:(3 + k) * size] = product(inv1, both[k]) / scaling
        for q in range(2):
            a2_copy(q).wait_send()

    g_drain_all(gram)
    y_drain()
    y_drain_all(mine_xy)
    swap_copy().wait_send()


def fused(columns):
    row_count = lax.axis_size("rows")
    width = columns.shape[1]
    scaling = math.sqrt(width * row_count)
    size = PANEL
    mates = row_count // 2
    f32 = jnp.float32
    vmem = pl.BlockSpec(memory_space=pltpu.VMEM)
    return pl.pallas_call(
        functools.partial(kernel, row_count, scaling),
        out_shape=(
            jax.ShapeDtypeStruct((size, width), f32),
            jax.ShapeDtypeStruct((size, 4 * size), f32),
            jax.ShapeDtypeStruct((size, width), f32),
        ),
        in_specs=[vmem],
        out_specs=(vmem, vmem, vmem),
        scratch_shapes=[
            pltpu.VMEM((2 * size, width), f32),
            pltpu.VMEM((size, width), f32),
            pltpu.VMEM((3 * size, size), f32),
            pltpu.VMEM((3 * size, size), f32),
            pltpu.VMEM((3 * size // 2, size), f32),
            pltpu.VMEM((mates, 3 * size // row_count, size), f32),
            pltpu.VMEM((2, 2 * size, size), f32),
            pltpu.VMEM((size, 3 * size), f32),
            pltpu.VMEM((size, 3 * size), f32),
            pltpu.VMEM((2 * size, size), f32),
            pltpu.VMEM((size, size), f32),
            pltpu.VMEM((mates, 2 * size // row_count, size), f32),
            pltpu.SemaphoreType.DMA((4 + 2 * (2 * mates + 2),)),
            pltpu.SemaphoreType.DMA((4,)),
            pltpu.SemaphoreType.DMA((2,)),
            pltpu.SemaphoreType.DMA((2 * mates,)),
            pltpu.SemaphoreType.DMA((2 * mates,)),
            pltpu.SemaphoreType.DMA((2,)),
            pltpu.SemaphoreType.DMA((2,)),
        ],
        compiler_params=pltpu.CompilerParams(collective_id=0, has_side_effects=True),
    )(columns)


def inverse_lower(lower):
    identity = jnp.eye(lower.shape[0], dtype=lower.dtype)
    return lax.linalg.triangular_solve(lower, identity, left_side=True, lower=True)


def summed(partial_term):
    return lax.psum(partial_term, "rows")


def general(columns):
    col_count = lax.axis_size("cols")
    col_index = lax.axis_index("cols")
    scaling = math.sqrt(columns.shape[1] * lax.axis_size("rows"))
    local_rows = lax.all_gather(columns, "cols", axis=0, tiled=True)
    panel_count = 2 * PANEL
    leading = local_rows[:panel_count]
    gram_strip = summed(product(leading, local_rows.T))
    lower_both = jnp.linalg.cholesky(gram_strip[:, :panel_count])
    inverse_both = inverse_lower(lower_both)
    orthonormal = product(inverse_both, leading)
    coupling = product(inverse_both, gram_strip[:, panel_count:])
    trailing = local_rows[panel_count:] - product(coupling.T, orthonormal)
    triangle = jnp.concatenate([lower_both.T, coupling], axis=1)
    orthonormal = orthonormal * scaling
    triangle = triangle / scaling

    def own(array):
        count = array.shape[0] // col_count
        return lax.dynamic_slice_in_dim(array, col_index * count, count, 0)

    return (own(orthonormal), own(triangle), own(trailing))


def shards(columns):
    rows = lax.axis_size("rows")
    paired = lax.axis_size("cols") == 2 and columns.shape[0] == 2 * PANEL
    if paired and rows % 2 == 0 and (2 * PANEL) % (8 * rows) == 0 and (3 * PANEL) % (8 * rows) == 0:
        return fused(columns)
    return general(columns)


def solution(mesh):
    placed = (P("cols", "rows"),)
    return jax.shard_map(
        shards,
        mesh=mesh,
        in_specs=placed,
        out_specs=(P("cols", "rows"), P("cols", None), P("cols", "rows")),
        check_vma=False,
    )
```

time: 216 us -> 54.6 us (0.25)
  waiting for transfers between devices: 129 us -> 0 us
  other arithmetic: 56.5 us -> 0 us
  Pallas kernels: 0 us -> 50.3 us
  between operations: 15.5 us -> 0.66 us
  matrix products: 8.32 us -> 0 us
  local copies, waits for them, and re-layouts: 5.99 us -> 3.46 us
    psum x1 -> x0, waiting for transfers between devices: 90.8 us -> none  [summed(): return lax.psum(partial_term, 'rows')]
    another operation x8 -> x0, other arithmetic: 53.7 us -> none  [the longest x6 34 us: shards(): lower_both = jnp.linalg.cholesky(gram_strip[:, :panel_count])]
    pallas_call x0 -> x1, Pallas kernels: none -> 50.3 us  [fused(): pl.pallas_call(functools.partial(kernel, row_count, scaling), out_shape=(...]
    all_gather x1 -> x0, waiting for transfers between devices: 37.4 us -> none  [shards(): local_rows = lax.all_gather(columns, 'cols', axis=0, tiled=True)]
    dot_general x4 -> x0, matrix products: 7.01 us -> none  [product(): jnp.dot(left, right, precision=precise, preferred_element_type=jnp.float32)]
    another operation x9 -> x0, local copies, waits for them, and re-layouts: 4.05 us -> none
    unnamed x5 -> x7, local copies, waits for them, and re-layouts: 0.85 us -> 3.46 us
  transfers between devices with their start and end apart: 2 -> 0, of which waited for: 2 -> 0; matrix products, arithmetic and copies ran while one was open for 0% -> 0% of each run, Pallas kernels for 0% -> 0%
where the time goes in v1:
time: 54.6 us; the launch traced here: 54.4 us
  Pallas kernels  50.3 us (92%)
  local copies, waits for them, and re-layouts  3.46 us (6%)
  between operations  0.66 us (1%)
    pallas_call x1, Pallas kernels, fused(): pl.pallas_call(functools.partial(kernel, row_count, scaling), out_shape=(...  50.3 us
    unnamed x7, local copies, waits for them, and re-layouts  3.46 us

profile of v1, /device:TPU:0, one launch (start us, length us, event | category | flops | bytes accessed | tf_op | source)
XLA Modules:
  0.0 54.4 jit_solution(9224301333571644047)
XLA Ops:
  0.6 50.3 %shard_map.38 = (f32[128,1024]{1,0:T(8,128)}, f32[128,512]{1,0:T(8,128)}, f32[128,1024]{1,0:T(8,128)}) custom-call(f32[256,1024]{1,0:T(8,128)} %x_ref.1), custom_call_target="tpu_custom_call" | custom-call | tf_op jit(solution)/shard_map/pallas_call | solution.py:346
  50.9 0.0 copy-start.1
  50.9 0.0 copy-start
  50.9 2.0 %copy.7 = f32[128,1024]{1,0:T(8,128)} copy(f32[128,1024]{1,0:T(8,128)} %get-tuple-element.6) | data formatting | bytes 1048576
  52.9 0.0 copy-done.1
  52.9 0.7 %copy.8 = f32[128,512]{1,0:T(8,128)} copy(f32[128,512]{1,0:T(8,128)S(1)} %copy-done.1) | data formatting | bytes 524288
  53.6 0.0 copy-done
  53.6 0.8 %copy.9 = f32[128,1024]{1,0:T(8,128)} copy(f32[128,1024]{1,0:T(8,128)S(1)} %copy-done) | data formatting | bytes 1048576
Async XLA Ops:
  50.9 2.0 %copy-start.1 = (f32[128,512]{1,0:T(8,128)S(1)}, f32[128,512]{1,0:T(8,128)}, u32[]{:S(2)}) copy-start(f32[128,512]{1,0:T(8,128)} %get-tuple-element.7) | copy-start | bytes 786436
  50.9 2.7 %copy-start = (f32[128,1024]{1,0:T(8,128)S(1)}, f32[128,1024]{1,0:T(8,128)}, u32[]{:S(2)}) copy-start(f32[128,1024]{1,0:T(8,128)} %get-tuple-element.8) | copy-start | bytes 1572868

commit v2 on v1

--- a/solution.py
+++ b/solution.py
@@ -81,9 +81,9 @@
 
 
 def kernel(row_count, scaling, x_ref, ortho_ref, tri_ref, trail_ref,
-           xs, a2, part, gram, pair_in, ring_in, both, first, second,
-           xy, xy_pair, xy_ring, send, recv_x, recv_pair, recv_ring, recv_all,
-           recv_half, recv_y):
+           xs, ys, qs, part, gram, pair_in, ring_in, first, second,
+           xy, xy_pair, xy_ring, xy_own, xy_other, coupled, send, recv_x, recv_pair,
+           recv_ring, recv_all, recv_half, recv_y):
     r = lax.axis_index("rows")
     c = lax.axis_index("cols")
     other = 1 - c
@@ -108,28 +108,29 @@
             src_ref=src, dst_ref=dst, send_sem=send_sem, recv_sem=recv_sem,
             device_id=target, device_id_type=MESH)
 
-    quarter = size // 2
+    width = x_ref.shape[1]
+    eighth = width // 8
+    early = pl.ds(0, 4 * eighth)
+    late = pl.ds(4 * eighth, 4 * eighth)
+    spans = ((4, 3), (7, 1), (0, 3), (3, 1))
 
     def x_copy(q):
-        return push(x_ref.at[pl.ds(q * quarter, quarter)],
-                    xs.at[pl.ds(q * quarter, quarter)],
-                    send.at[q], recv_x.at[q], across)
-
-    def a2_copy(q):
-        return push(x_ref.at[pl.ds(q * quarter, quarter)],
-                    a2.at[pl.ds(q * quarter, quarter)],
-                    send.at[q], recv_x.at[q], across)
+        span = pl.ds(spans[q][0] * eighth, spans[q][1] * eighth)
+        return push(x_ref.at[:, span], xs.at[:, span], send.at[q], recv_x.at[q], across)
+
+    def y_copy(q):
+        view = (pl.ds(0, 2 * size), early) if q == 0 else (pl.ds(0, size), late)
+        return push(x_ref.at[view], ys.at[view], send.at[q], recv_x.at[q], across)
 
     @pl.when(c == 0)
     def _():
         x_copy(0).start()
-        x_copy(1).start()
 
     @pl.when(c == 1)
     def _():
-        a2_copy(0).start()
-        a2_copy(1).start()
-        a2[...] = x_ref[size:, :]
+        y_copy(0).start()
+        y_copy(1).start()
+        ys[...] = x_ref[...]
 
     def spread(base, full, pair_buf, ring_buf, tag):
         half = full.shape[0] // 2
@@ -175,13 +176,13 @@
             for k in range(1, mates):
                 ring_copy(k).start()
 
-        def finish_ring(dst):
+        def finish_ring():
             for k in range(1, mates):
                 ring_copy(k).wait_recv()
             total = full[own]
             for k in range(1, mates):
                 total = total + ring_buf[k]
-            dst[own] = total
+            return total
 
         def drain_scatter():
             pair_copy().wait_send()
@@ -217,19 +218,22 @@
     def chunk_copy():
         return push(gram.at[g_own], gram.at[g_own], y_send, recv_y.at[0], across)
 
+    (y_pair, y_ring, y_sum, y_drain, y_gather, y_half, y_finish, y_drain_all,
+     y_own) = spread(base_y, xy, xy_pair, xy_ring, 1)
+
     @pl.when(c == 0)
     def _():
-        part[:2 * size] = across_rows(x_ref[...], x_ref[:size])
+        strip = across_rows(x_ref[:size], x_ref[...])
+        part[:size] = strip[:, :size]
+        part[size:2 * size] = strip[:, size:]
         part[2 * size:] = across_rows(x_ref[size:, :], x_ref[size:, :])
-        low = part[size:2 * size]
-        part[size:2 * size] = low.T
         g_pair()
         xs[...] = x_ref[...]
         g_ring()
-        g_sum(gram)
+        gram[g_own] = g_sum()
         chunk_copy().start()
+        x_copy(1).start()
         x_copy(2).start()
-        x_copy(3).start()
 
     @pl.when(c == 1)
     def _():
@@ -237,6 +241,19 @@
 
     g_gather(gram)
     g_half(gram)
+
+    @pl.when(c == 0)
+    def _():
+        y_copy(0).wait_recv()
+        xy[...] = across_rows(xs[:, early], ys[:, early])
+
+    @pl.when(c == 1)
+    def _():
+        x_copy(0).wait_recv()
+        x_copy(1).wait_recv()
+        xy[...] = across_rows(xs[:, late], ys[:, late])
+
+    y_pair()
     g_finish(gram)
 
     eye = (lax.broadcasted_iota(jnp.int32, (size, size), 0)
@@ -244,67 +261,53 @@
     first[:, :size] = gram[:size]
     first[:, size:2 * size] = gram[size:2 * size]
     first[:, 2 * size:] = eye
-    eliminate(first, {})
-
-    @pl.when(c == 0)
-    def _():
-        a2_copy(0).wait_recv()
-        a2_copy(1).wait_recv()
-
-    @pl.when(c == 1)
-    def _():
-        for q in range(4):
-            x_copy(q).wait_recv()
-
-    (y_pair, y_ring, y_sum, y_drain, y_gather, y_half, y_finish, y_drain_all,
-     _own) = spread(base_y, xy, xy_pair, xy_ring, 1)
-    xy[...] = across_rows(xs[...], a2[...])
-    y_pair()
+
+    def swap_copy():
+        return push(xy_own, xy_other, send.at[base_y + 2 * mates + 1], recv_y.at[1], across)
+
+    def hook_sum():
+        xy_own[...] = y_sum()
+        swap_copy().start()
+
+        @pl.when(c == 0)
+        def _():
+            x_copy(3).start()
+
+    def hook_gather():
+        swap_copy().wait_recv()
+        coupled[y_own] = xy_own[...] + xy_other[...]
+        y_gather(coupled)
+
+    eliminate(first, {0: y_ring, 6: hook_sum})
 
     upper = first[:, size:2 * size]
     cross = contract(upper, first[:, size:], ((0,), (0,)))
     second[:, :size] = gram[2 * size:] - cross[:, :size]
     second[:, size:2 * size] = -cross[:, size:]
     second[:, 2 * size:] = eye
-
-    mine_xy = both.at[c]
-
-    def swap_copy():
-        return push(both.at[c], both.at[c], send.at[base_y + 2 * mates + 1],
-                    recv_y.at[1], across)
-
-    def swap_wait():
-        push(both.at[other], both.at[other], send.at[base_y + 2 * mates + 1],
-             recv_y.at[1], across).wait_recv()
-
-    def hook_sum():
-        y_sum(mine_xy)
-        y_gather(mine_xy)
-
-    def hook_swap():
-        y_finish(mine_xy)
-        swap_copy().start()
-
-    eliminate(second, {0: y_ring, 3: hook_sum, 6: lambda: y_half(mine_xy), 7: hook_swap})
+    eliminate(second, {0: hook_gather, 7: lambda: y_half(coupled)})
+
+    @pl.when(c == 1)
+    def _():
+        x_copy(2).wait_recv()
+        x_copy(3).wait_recv()
 
     inv00 = first[:, 2 * size:]
     inv1 = second[:, size:]
-    mine = both[c]
-    coup0 = product(inv00, mine[:size])
-    coup1 = product(inv1, mine)
-    weights = contract(coup1, inv1, ((0,), (0,)))
-    weights0 = weights[:, :size] + contract(coup0, inv00, ((0,), (0,)))
-    trail_ref[...] = a2[...] - (product(weights0, xs[:size]) + product(weights[:, size:], xs[size:]))
+    qs[:size] = product(inv00, xs[:size])
+    qs[size:] = product(inv1, xs[...])
+    own_rows = pl.ds(pl.multiple_of(c * size, size), size)
+    ortho_ref[...] = qs[own_rows] * scaling
 
     @pl.when(c == 0)
     def _():
-        ortho_ref[...] = product(inv00, xs[:size]) * scaling
-
-    @pl.when(c == 1)
-    def _():
-        ortho_ref[...] = product(inv1, xs[...]) * scaling
-
-    swap_wait()
+        y_copy(1).wait_recv()
+
+    y_finish(coupled)
+    mine = coupled[:, pl.ds(pl.multiple_of(c * size, size), size)]
+    coup = jnp.concatenate([product(inv00, mine[:size]), product(inv1, mine)], axis=0)
+    trail_ref[...] = ys[own_rows] - contract(coup, qs[...], ((0,), (0,)))
+
     keep = (lax.broadcasted_iota(jnp.int32, (size, size), 0)
             <= lax.broadcasted_iota(jnp.int32, (size, size), 1))
 
@@ -312,9 +315,7 @@
     def _():
         tri_ref[:, :size] = jnp.where(keep, first[:, :size], 0.0) / scaling
         tri_ref[:, size:2 * size] = first[:, size:2 * size] / scaling
-        for k in range(2):
-            tri_ref[:, (2 + k) * size:(3 + k) * size] = (
-                product(inv00, both[k][:size]) / scaling)
+        tri_ref[:, 2 * size:] = product(inv00, coupled[:size]) / scaling
         for q in range(4):
             x_copy(q).wait_send()
         g_drain()
@@ -324,14 +325,13 @@
     def _():
         tri_ref[:, :size] = jnp.zeros((size, size), jnp.float32)
         tri_ref[:, size:2 * size] = jnp.where(keep, second[:, :size], 0.0) / scaling
-        for k in range(2):
-            tri_ref[:, (2 + k) * size:(3 + k) * size] = product(inv1, both[k]) / scaling
+        tri_ref[:, 2 * size:] = product(inv1, coupled[...]) / scaling
         for q in range(2):
-            a2_copy(q).wait_send()
+            y_copy(q).wait_send()
 
     g_drain_all(gram)
     y_drain()
-    y_drain_all(mine_xy)
+    y_drain_all(coupled)
     swap_copy().wait_send()
 
 
@@ -354,17 +354,20 @@
         out_specs=(vmem, vmem, vmem),
         scratch_shapes=[
             pltpu.VMEM((2 * size, width), f32),
-            pltpu.VMEM((size, width), f32),
+            pltpu.VMEM((2 * size, width), f32),
+            pltpu.VMEM((2 * size, width), f32),
             pltpu.VMEM((3 * size, size), f32),
             pltpu.VMEM((3 * size, size), f32),
             pltpu.VMEM((3 * size // 2, size), f32),
             pltpu.VMEM((mates, 3 * size // row_count, size), f32),
-            pltpu.VMEM((2, 2 * size, size), f32),
             pltpu.VMEM((size, 3 * size), f32),
             pltpu.VMEM((size, 3 * size), f32),
-            pltpu.VMEM((2 * size, size), f32),
-            pltpu.VMEM((size, size), f32),
-            pltpu.VMEM((mates, 2 * size // row_count, size), f32),
+            pltpu.VMEM((2 * size, 2 * size), f32),
+            pltpu.VMEM((size, 2 * size), f32),
+            pltpu.VMEM((mates, 2 * size // row_count, 2 * size), f32),
+            pltpu.VMEM((2 * size // row_count, 2 * size), f32),
+            pltpu.VMEM((2 * size // row_count, 2 * size), f32),
+            pltpu.VMEM((2 * size, 2 * size), f32),
             pltpu.SemaphoreType.DMA((4 + 2 * (2 * mates + 2),)),
             pltpu.SemaphoreType.DMA((4,)),
             pltpu.SemaphoreType.DMA((2,)),
@@ -412,7 +415,7 @@
 
 def shards(columns):
     rows = lax.axis_size("rows")
-    paired = lax.axis_size("cols") == 2 and columns.shape[0] == 2 * PANEL
+    paired = lax.axis_size("cols") == 2 and columns.shape[0] == 2 * PANEL and columns.shape[1] % (8 * PANEL) == 0
     if paired and rows % 2 == 0 and (2 * PANEL) % (8 * rows) == 0 and (3 * PANEL) % (8 * rows) == 0:
         return fused(columns)
     return general(columns)

time: 54.6 us -> 44.1 us (0.81)
  Pallas kernels: 50.3 us -> 39.8 us
    pallas_call x1, Pallas kernels: 50.3 us -> 39.8 us  [fused(): pl.pallas_call(functools.partial(kernel, row_count, scaling), out_shape=(...]
where the time goes in v2:
time: 44.1 us; the launch traced here: 44 us
  Pallas kernels  39.8 us (90%)
  local copies, waits for them, and re-layouts  3.46 us (8%)
  between operations  0.66 us (1%)
    pallas_call x1, Pallas kernels, fused(): pl.pallas_call(functools.partial(kernel, row_count, scaling), out_shape=(...  39.8 us
    unnamed x7, local copies, waits for them, and re-layouts  3.46 us

profile of v2, /device:TPU:0, one launch (start us, length us, event | category | flops | bytes accessed | tf_op | source)
XLA Modules:
  0.0 44.0 jit_solution(14381784599933878966)
XLA Ops:
  0.6 39.8 %shard_map.38 = (f32[128,1024]{1,0:T(8,128)}, f32[128,512]{1,0:T(8,128)}, f32[128,1024]{1,0:T(8,128)}) custom-call(f32[256,1024]{1,0:T(8,128)} %x_ref.1), custom_call_target="tpu_custom_call" | custom-call | tf_op jit(solution)/shard_map/pallas_call | solution.py:346
  40.5 0.0 copy-start.1
  40.5 0.0 copy-start
  40.5 2.0 %copy.7 = f32[128,1024]{1,0:T(8,128)} copy(f32[128,1024]{1,0:T(8,128)} %get-tuple-element.6) | data formatting | bytes 1048576
  42.5 0.0 copy-done.1
  42.5 0.7 %copy.8 = f32[128,512]{1,0:T(8,128)} copy(f32[128,512]{1,0:T(8,128)S(1)} %copy-done.1) | data formatting | bytes 524288
  43.2 0.0 copy-done
  43.2 0.8 %copy.9 = f32[128,1024]{1,0:T(8,128)} copy(f32[128,1024]{1,0:T(8,128)S(1)} %copy-done) | data formatting | bytes 1048576
Async XLA Ops:
  40.5 2.0 %copy-start.1 = (f32[128,512]{1,0:T(8,128)S(1)}, f32[128,512]{1,0:T(8,128)}, u32[]{:S(2)}) copy-start(f32[128,512]{1,0:T(8,128)} %get-tuple-element.7) | copy-start | bytes 786436
  40.5 2.7 %copy-start = (f32[128,1024]{1,0:T(8,128)S(1)}, f32[128,1024]{1,0:T(8,128)}, u32[]{:S(2)}) copy-start(f32[128,1024]{1,0:T(8,128)} %get-tuple-element.8) | copy-start | bytes 1572868

commit v3 on v2

--- a/solution.py
+++ b/solution.py
@@ -10,6 +10,7 @@
 
 PANEL = 128
 STRIP = 16
+VMEM_BYTES = 20 * 2**20
 MESH = pl.DeviceIdType.MESH
 
 precise = lax.Precision.HIGHEST
@@ -80,8 +81,8 @@
             hooks[s]()
 
 
-def kernel(row_count, scaling, x_ref, ortho_ref, tri_ref, trail_ref,
-           xs, ys, qs, part, gram, pair_in, ring_in, first, second,
+def kernel(row_count, scaling, x_ref, qs, tri_ref, tail_ref, coup_ref,
+           xs, ys, part, gram, pair_in, ring_in, first, second,
            xy, xy_pair, xy_ring, xy_own, xy_other, coupled, send, recv_x, recv_pair,
            recv_ring, recv_all, recv_half, recv_y):
     r = lax.axis_index("rows")
@@ -297,16 +298,16 @@
     qs[:size] = product(inv00, xs[:size])
     qs[size:] = product(inv1, xs[...])
     own_rows = pl.ds(pl.multiple_of(c * size, size), size)
-    ortho_ref[...] = qs[own_rows] * scaling
 
     @pl.when(c == 0)
     def _():
         y_copy(1).wait_recv()
 
+    tail_ref[...] = ys[own_rows]
     y_finish(coupled)
     mine = coupled[:, pl.ds(pl.multiple_of(c * size, size), size)]
-    coup = jnp.concatenate([product(inv00, mine[:size]), product(inv1, mine)], axis=0)
-    trail_ref[...] = ys[own_rows] - contract(coup, qs[...], ((0,), (0,)))
+    coup_ref[:size] = product(inv00, mine[:size])
+    coup_ref[size:] = product(inv1, mine)
 
     keep = (lax.broadcasted_iota(jnp.int32, (size, size), 0)
             <= lax.broadcasted_iota(jnp.int32, (size, size), 1))
@@ -333,6 +334,17 @@
     y_drain()
     y_drain_all(coupled)
     swap_copy().wait_send()
+
+
+def finish_kernel(scaling, q_ref, tri_in, tail_in, coup_ref, ortho_ref, tri_ref, trail_ref):
+    size = coup_ref.shape[1]
+    own_rows = pl.ds(pl.multiple_of(lax.axis_index("cols") * size, size), size)
+    ortho_ref[...] = q_ref[own_rows] * scaling
+    trail_ref[...] = tail_in[...] - contract(coup_ref[...], q_ref[...], ((0,), (0,)))
+
+    @pl.when(pl.program_id(0) == 0)
+    def _():
+        tri_ref[...] = tri_in[...]
 
 
 def fused(columns):
@@ -343,17 +355,20 @@
     mates = row_count // 2
     f32 = jnp.float32
     vmem = pl.BlockSpec(memory_space=pltpu.VMEM)
-    return pl.pallas_call(
+    ortho = jax.ShapeDtypeStruct((size, width), f32)
+    triangle = jax.ShapeDtypeStruct((size, 4 * size), f32)
+    trailing = ortho
+    middle = pl.pallas_call(
         functools.partial(kernel, row_count, scaling),
         out_shape=(
-            jax.ShapeDtypeStruct((size, width), f32),
-            jax.ShapeDtypeStruct((size, 4 * size), f32),
-            jax.ShapeDtypeStruct((size, width), f32),
+            jax.ShapeDtypeStruct((2 * size, width), f32),
+            triangle,
+            trailing,
+            jax.ShapeDtypeStruct((2 * size, size), f32),
         ),
         in_specs=[vmem],
-        out_specs=(vmem, vmem, vmem),
+        out_specs=(vmem, vmem, vmem, vmem),
         scratch_shapes=[
-            pltpu.VMEM((2 * size, width), f32),
             pltpu.VMEM((2 * size, width), f32),
             pltpu.VMEM((2 * size, width), f32),
             pltpu.VMEM((3 * size, size), f32),
@@ -376,8 +391,26 @@
             pltpu.SemaphoreType.DMA((2,)),
             pltpu.SemaphoreType.DMA((2,)),
         ],
-        compiler_params=pltpu.CompilerParams(collective_id=0, has_side_effects=True),
+        compiler_params=pltpu.CompilerParams(
+            collective_id=0, has_side_effects=True, vmem_limit_bytes=VMEM_BYTES),
     )(columns)
+    steps = 2
+    span = width // steps
+
+    def along(rows):
+        return pl.BlockSpec((rows, span), lambda i: (0, i))
+
+    def whole(shape):
+        return pl.BlockSpec(shape, lambda i: (0, 0))
+
+    return pl.pallas_call(
+        functools.partial(finish_kernel, scaling),
+        grid=(steps,),
+        out_shape=(ortho, triangle, trailing),
+        in_specs=[along(2 * size), whole(triangle.shape), along(size), whole((2 * size, size))],
+        out_specs=(along(size), whole(triangle.shape), along(size)),
+        compiler_params=pltpu.CompilerParams(vmem_limit_bytes=VMEM_BYTES),
+    )(*middle)
 
 
 def inverse_lower(lower):

time: 44.1 us -> 40.9 us (0.927)
  local copies, waits for them, and re-layouts: 3.46 us -> 1.22 us
  Pallas kernels: 39.8 us -> 38.9 us
    pallas_call x1, Pallas kernels: 39.8 us -> 36.9 us  [fused(): pl.pallas_call(functools.partial(kernel, row_count, scaling), out_shape=(...]
    unnamed x7 -> x2, local copies, waits for them, and re-layouts: 3.46 us -> 1.22 us
    pallas_call x0 -> x1, Pallas kernels: none -> 1.97 us  [fused(): pl.pallas_call(functools.partial(finish_kernel, scaling), grid=(steps,),...]
where the time goes in v3:
time: 40.9 us; the launch traced here: 40.7 us
  Pallas kernels  38.9 us (95%)
  local copies, waits for them, and re-layouts  1.22 us (3%)
  between operations  0.65 us (2%)
    pallas_call x1, Pallas kernels, fused(): pl.pallas_call(functools.partial(kernel, row_count, scaling), out_shape=(...  36.9 us
    pallas_call x1, Pallas kernels, fused(): pl.pallas_call(functools.partial(finish_kernel, scaling), grid=(steps,),...  1.97 us
    unnamed x2, local copies, waits for them, and re-layouts  1.22 us

profile of v3, /device:TPU:0, one launch (start us, length us, event | category | flops | bytes accessed | tf_op | source)
XLA Modules:
  0.0 40.7 jit_solution(1021343798852764630)
XLA Ops:
  0.6 0.0 copy-start
  0.6 1.2 %copy-done = f32[256,1024]{1,0:T(8,128)S(1)} copy-done((f32[256,1024]{1,0:T(8,128)S(1)}, f32[256,1024]{1,0:T(8,128)}, u32[]{:S(2)}) %copy-start) | copy-done | bytes 1048600
  1.9 36.9 %shard_map.38 = (f32[256,1024]{1,0:T(8,128)S(1)}, f32[128,512]{1,0:T(8,128)S(1)}, f32[128,1024]{1,0:T(8,128)S(1)}, f32[256,128]{1,0:T(8,128)S(1)}) custom-call(f32[256,1024]{1,0:T(8,128)S(1)} %copy-done), custom_call_target="tpu_custom_call" | custom-call | tf_op jit(solution)/shard_map/pallas_call | solution.py:361
  38.7 2.0 %shard_map.39 = (f32[128,1024]{1,0:T(8,128)}, f32[128,512]{1,0:T(8,128)}, f32[128,1024]{1,0:T(8,128)}) custom-call(f32[256,1024]{1,0:T(8,128)S(1)} %get-tuple-element.7.q_ref, f32[128,512]{1,0:T(8,128)S(1)} %get-tuple-element.8.tri_in, f32[128,1024]{1,0:T(8,128)S(1)} %get-tuple-element.9.tail_in, f32[256,128]{1,0:T(8,128)S(1)} %get-tuple-element.10.coup_ref), custom_call_target="tpu_custom_call" | custom-call | tf_op jit(solution)/shard_map/pallas_call | solution.py:406
Async XLA Ops:
  0.6 1.2 %copy-start = (f32[256,1024]{1,0:T(8,128)S(1)}, f32[256,1024]{1,0:T(8,128)}, u32[]{:S(2)}) copy-start(f32[256,1024]{1,0:T(8,128)} %x_ref.1) | copy-start | bytes 3145732
